TPU v7x, 32 devices: a whole 2x2x4 slice. The times are simulated.
32 devices in a mesh: grp: 2 (over x), path: 8 (over z, y), amp: 2 (over core).
Axes of the slice: x: 2, y: 2, z: 4, core: 2. Of those that a mesh axis runs over, the one named last changes fastest.
Arguments:
- left_slabs: bfloat16 [256, 2, 16384], P(('grp', 'path'), None, 'amp'), parts along dimension 0, may hold values from -0.59765625 to 0.59765625
- right_slabs: bfloat16 [256, 2, 8192], P(('grp', 'path'), None, 'amp'), parts along dimension 0, may hold values from -0.59765625 to 0.59765625
- term_index: int32 [256], P(('grp', 'path')), parts along dimension 0, may hold values from 0 to 3
- left_terms: float32 [4, 2, 2, 2], replicated, may hold values from -4.2 to 4.2
- right_terms: float32 [4, 2, 2, 2], replicated, may hold values from -4.2 to 4.2
- left_gates: bfloat16 [2, 2, 128, 128], replicated, may hold values from -0.375 to 0.375
- right_gates: bfloat16 [2, 2, 128, 128], replicated, may hold values from -0.375 to 0.375
Outputs:
- amplitudes: bfloat16 [2, 32768, 8192], P(None, ('grp', 'path'), 'amp'), parts along dimension 1
There are 2 independent parts, one for each index of `grp`. A program takes and returns all parts, laid end to end along the dimension named above; an argument that names none is the same for every part. Nothing has to cross between parts.
All inputs are finite; a program needn't handle non-finite values.
Results may differ from a plain program's by a relative error of at most 0.0081.
Values may be sent and summed in bfloat16 or wider, within the bound.
No kernel may reach another device: no remote copies, remote signals or barrier semaphores. Data moves between devices by JAX's collectives and lax.ppermute only.
A program may use at most 128 MiB of HBM per device.

v0:
```python
import jax
import jax.numpy as jnp
from jax import lax
from jax.sharding import PartitionSpec as P


def cut_term(slab, term_mix):
    paths_here, _, length = slab.shape
    width = min(128, length)
    values = slab.astype(jnp.float32).reshape(paths_here, 2, length // width, width)
    identity = jnp.eye(width // 2, dtype=jnp.float32)

    def expand(part):
        return jnp.einsum("ab,nmj->najbm", identity, part).reshape(paths_here, width, width)

    real_kron = expand(term_mix[:, 0])
    imag_kron = expand(term_mix[:, 1])
    batch_dims = (((2,), (1,)), ((0,), (0,)))

    def times(rows, kron):
        return lax.dot_general(
            rows,
            kron,
            batch_dims,
            precision=lax.Precision.HIGHEST,
            preferred_element_type=jnp.float32,
        )

    real_rows = values[:, 0]
    imag_rows = values[:, 1]
    real_part = times(real_rows, real_kron) - times(imag_rows, imag_kron)
    imag_part = times(real_rows, imag_kron) + times(imag_rows, real_kron)
    return jnp.stack([real_part, imag_part], 1).reshape(paths_here, 2, length).astype(jnp.bfloat16)


def apply_low(slab, gate_mat):
    paths_here, _, length = slab.shape
    gate_width = gate_mat.shape[-1]
    real_rows = slab[:, 0].reshape(-1, gate_width)
    imag_rows = slab[:, 1].reshape(-1, gate_width)
    upper = jnp.concatenate([gate_mat[0].T, gate_mat[1].T], 1)
    lower = jnp.concatenate([-gate_mat[1].T, gate_mat[0].T], 1)
    right_matrix = jnp.concatenate([upper, lower], 0)
    product = jnp.dot(
        jnp.concatenate([real_rows, imag_rows], 1), right_matrix, preferred_element_type=jnp.float32
    )
    real_part = product[:, :gate_width].reshape(paths_here, length)
    imag_part = product[:, gate_width:].reshape(paths_here, length)
    return jnp.stack([real_part, imag_part], 1).astype(jnp.bfloat16)


def stack_matrix(gate_mat):
    upper = jnp.concatenate([gate_mat[0], -gate_mat[1]], 1)
    lower = jnp.concatenate([gate_mat[1], gate_mat[0]], 1)
    return jnp.concatenate([upper, lower], 0)


def gate_rows(matrix, data):
    batch = jnp.broadcast_to(matrix, (data.shape[0],) + matrix.shape)
    return lax.dot_general(
        batch, data, (((2,), (1,)), ((0,), (0,))), preferred_element_type=jnp.float32
    )


def right_high(moved, gate_mat):
    half_paths = moved.shape[0]
    gate_width = gate_mat.shape[-1]
    low_width = gate_width // 2
    data = moved.reshape(half_paths, gate_width, gate_width)
    blocks = gate_mat.reshape(2, low_width, 2, low_width, 2)
    rows_index = jnp.arange(gate_width, dtype=jnp.int32)[:, None]
    cols_index = jnp.arange(gate_width, dtype=jnp.int32)[None, :]
    same_slot = rows_index % low_width == cols_index % low_width
    total = jnp.zeros((half_paths, gate_width, gate_width), jnp.float32)
    for target in range(2):
        for source in range(2):
            select = (
                same_slot
                & (rows_index // low_width == source)
                & (cols_index // low_width == target)
            ).astype(jnp.bfloat16)
            placed = jnp.dot(
                data.reshape(-1, gate_width), select, preferred_element_type=jnp.float32
            )
            placed = placed.astype(jnp.bfloat16).reshape(half_paths, gate_width, gate_width)
            matrix = stack_matrix(blocks[:, :, target, :, source])
            total = total + gate_rows(matrix, placed)
    return total.astype(jnp.bfloat16).reshape(half_paths, 2, -1)


def contract(left_part, right_part):
    left_stack = jnp.concatenate([left_part[:, 0], left_part[:, 1]], 0)
    right_real = jnp.concatenate([right_part[:, 0], -right_part[:, 1]], 0)
    right_imag = jnp.concatenate([right_part[:, 1], right_part[:, 0]], 0)
    contract_dims = (((0,), (0,)), ((), ()))
    real_part = lax.dot_general(
        left_stack, right_real, contract_dims, preferred_element_type=jnp.float32
    )
    imag_part = lax.dot_general(
        left_stack, right_imag, contract_dims, preferred_element_type=jnp.float32
    )
    return (real_part, imag_part)


def mixes(term_index, terms):
    chosen = (term_index[:, None] == jnp.arange(terms.shape[0], dtype=jnp.int32)[None, :]).astype(
        jnp.float32
    )
    flat = jnp.dot(chosen, terms.reshape(terms.shape[0], 8), precision=lax.Precision.HIGHEST)
    return flat.reshape(-1, 2, 2, 2)


def shards(left_slabs, right_slabs, term_index, left_terms, right_terms, left_gates, right_gates):
    gate_width = left_gates.shape[-1]
    path_count = lax.axis_size("path")
    left = cut_term(left_slabs, mixes(term_index, left_terms))
    left = apply_low(left, left_gates[0])
    moved = lax.all_to_all(left, "amp", split_axis=0, concat_axis=2, tiled=True)
    half_paths = moved.shape[0]
    full_left = moved.shape[2]
    turned = gate_rows(
        stack_matrix(left_gates[1]),
        moved.reshape(half_paths, 2 * gate_width, full_left // gate_width),
    )
    turned = turned.astype(jnp.bfloat16).reshape(half_paths, 2, full_left)
    portion = lax.all_to_all(turned, "path", split_axis=2, concat_axis=0, tiled=True)
    rows_here = portion.shape[2]
    portion = portion.reshape(path_count, half_paths, 2, rows_here)
    row_block = lax.all_gather(portion, "amp", axis=1, tiled=True).reshape(
        path_count * half_paths * 2, 2, rows_here
    )
    right = cut_term(right_slabs, mixes(term_index, right_terms))
    right = apply_low(right, right_gates[0])
    right_moved = lax.all_to_all(right, "amp", split_axis=0, concat_axis=2, tiled=True)
    right_turned = right_high(right_moved, right_gates[1])
    right = lax.all_to_all(right_turned, "amp", split_axis=2, concat_axis=0, tiled=True)
    everything = lax.all_gather(right, "path", axis=0, tiled=True)
    real_part, imag_part = contract(row_block, everything)
    return jnp.stack([real_part, imag_part], 0).astype(jnp.bfloat16)


def solution(mesh):
    return jax.shard_map(
        shards,
        mesh=mesh,
        in_specs=(
            P(("grp", "path"), None, "amp"),
            P(("grp", "path"), None, "amp"),
            P(("grp", "path")),
            P(),
            P(),
            P(),
            P(),
        ),
        out_specs=P(None, ("grp", "path"), "amp"),
        check_vma=False,
    )
```

profile of v0, /device:TPU:0, one launch (start us, length us, event | category | flops | bytes accessed | tf_op | source)
XLA Modules:
  0.0 288.8 jit_solution(7753225383539384605)
XLA Ops:
  7.3 0.8 slice_bitcast_fusion.20
  9.0 0.8 fusion.66
  9.8 1.4 reshape.234
  11.3 18.8 %broadcast_multiply_fusion.3 = (f32[16,2,2,64,64]{0,1,4,2,3:T(2,128)}, f32[16,2,2,64,64]{0,1,4,2,3:T(2,128)}, f32[16,2,2,64,64]{0,1,4,2,3:T(2,128)}, f32[16,2,2,64,64]{0,1,4,2,3:T(2,128)}) fusion(f32[64,64]{1,0:T(8,128)S(1)} %fusion.61, f32[16,2,2]{0,1,2:T(2,128)S(1)} %copy.56, f32[16,2,2]{0,1,2:T(2,128)S(1)} %copy.59, f32[16,2,2]{0,1,2:T(2,128)S(1)} %copy.69, ...), kind=kLoop, calls=%fused_computation.6 | loop fusion | flops 1048576 | bytes 4211712 | tf_op jit(solution)/shard_map/ab,nmj->najbm/dot_general | solution.py:14
  30.1 5.2 %copy.58 = f32[16,128,128]{2,1,0:T(8,128)S(1)} copy(f32[16,128,128]{0,2,1:T(8,128)} %bitcast.165) | data formatting | bytes 2097152 | tf_op jit(solution)/shard_map/reshape | solution.py:14
  35.3 5.2 %copy.60 = f32[16,128,128]{2,1,0:T(8,128)S(1)} copy(f32[16,128,128]{0,2,1:T(8,128)} %bitcast.164) | data formatting | bytes 2097152 | tf_op jit(solution)/shard_map/reshape | solution.py:14
  43.8 2.0 pad_maximum_fusion.4
  45.8 3.7 %all-to-all-start = ((bf16[16,2,8192]{2,1,0:T(2,128)(2,1)}), bf16[16,2,8192]{2,1,0:T(2,128)(2,1)S(1)}, u32[]{:S(2)}, u32[]{:S(2)}) async-start(bf16[16,2,8192]{2,1,0:T(2,128)(2,1)} %pad_maximum_fusion.4), calls=%async_computation | async-start | bytes 1048576 | tf_op jit(solution)/shard_map/all_to_all | solution.py:118
  50.5 10.0 %reshape_squeeze.17 = bf16[2,64,2,64,2]{4,3,2,1,0:T(8,128)(2,1)} reshape(bf16[1,2,128,128]{3,2,1,0:T(8,128)(2,1)S(1)} %slice-done) | data formatting | bytes 131072 | tf_op jit(solution)/shard_map/reshape;squeeze | solution.py:70
  60.5 7.9 %slice_reduce_fusion = (bf16[64,64]{1,0:T(8,128)(2,1)S(1)}, bf16[64,64]{1,0:T(8,128)(2,1)S(1)}, bf16[64,64]{1,0:T(8,128)(2,1)S(1)}, bf16[64,64]{1,0:T(8,128)(2,1...) fusion(bf16[2,64,2,64,2]{4,3,2,1,0:T(8,128)(2,1)} %reshape_sque, ...), kind=kLoop, calls=%fused_computation.34 | loop fusion | bytes 131072 | tf_op jit(solution)/shard_map/slice | solution.py:53
  68.5 5.2 %copy.71 = f32[16,128,128]{2,1,0:T(8,128)S(1)} copy(f32[16,128,128]{0,2,1:T(8,128)} %bitcast.163) | data formatting | bytes 2097152 | tf_op jit(solution)/shard_map/reshape | solution.py:14
  73.8 5.2 %copy.73 = f32[16,128,128]{2,1,0:T(8,128)S(1)} copy(f32[16,128,128]{0,2,1:T(8,128)} %bitcast.162) | data formatting | bytes 2097152 | tf_op jit(solution)/shard_map/reshape | solution.py:14
  81.9 1.3 pad_maximum_fusion.5
  83.2 3.4 %all-to-all-start.2 = ((bf16[16,2,4096]{2,1,0:T(2,128)(2,1)}), bf16[16,2,4096]{2,1,0:T(2,128)(2,1)S(1)}, u32[]{:S(2)}, u32[]{:S(2)}) async-start(bf16[16,2,4096]{2,1,0:T(2,128)(2,1)} %pad_maximum_fusion.5), calls=%async_computation.2 | async-start | bytes 524288 | tf_op jit(solution)/shard_map/all_to_all | solution.py:134
  88.2 12.8 %copy.66 = bf16[8,2,16384]{0,1,2:T(2,128)(2,1)} copy(bf16[8,2,16384]{2,1,0:T(2,128)(2,1)S(1)} %reshape.222) | data formatting | bytes 1048576 | tf_op jit(solution)/shard_map/reshape | solution.py:125
  100.9 11.1 %reshape.246 = bf16[8,2,16384]{2,1,0:T(2,128)(2,1)} reshape(bf16[16384,2,8]{2,1,0:T(2,128)(2,1)} %bitcast.160) | data formatting | bytes 1048576
  112.1 7.3 %all-to-all-start.1 = ((bf16[8,2,16384]{2,1,0:T(2,128)(2,1)}), bf16[8,2,16384]{2,1,0:T(2,128)(2,1)S(1)}, u32[]{:S(2)}, u32[]{:S(2)}) async-start(bf16[8,2,16384]{2,1,0:T(2,128)(2,1)} %reshape.246), calls=%async_computation.1 | async-start | bytes 1048576 | tf_op jit(solution)/shard_map/all_to_all | solution.py:126
  121.6 12.9 %all-to-all-done.1 = bf16[8,2,16384]{2,1,0:T(2,128)(2,1)S(1)} async-done(((bf16[8,2,16384]{2,1,0:T(2,128)(2,1)}), bf16[8,2,16384]{2,1,0:T(2,128)(2,1)S(1)}, u32[]{:S(2)}, u32[]{:S(2)}) %all-to-all-start.1) | async-done | bytes 524320 | tf_op jit(solution)/shard_map/all_to_all | solution.py:126
  134.5 10.9 %reshape.247 = bf16[16384,2,8]{2,1,0:T(2,128)(2,1)} reshape(bf16[8,2,16384]{2,1,0:T(2,128)(2,1)S(1)} %all-to-all-done.1) | data formatting | bytes 1048576
  145.4 12.5 %copy.85 = bf16[8,2,8,2048]{3,2,0,1:T(8,128)(2,1)} copy(bf16[8,2,8,2048]{0,1,3,2:T(2,128)(2,1)} %bitcast.161) | data formatting | bytes 1048576 | tf_op jit(solution)/shard_map/all_to_all | solution.py:126
  159.1 6.8 %copy.80 = bf16[8,2,8192]{0,1,2:T(2,128)(2,1)} copy(bf16[8,2,8192]{2,1,0:T(2,128)(2,1)S(1)} %reshape.232) | data formatting | bytes 524288 | tf_op jit(solution)/shard_map/reshape | solution.py:88
  165.9 6.1 %reshape.244 = bf16[2,2,32768]{2,1,0:T(2,128)(2,1)S(1)} reshape(bf16[8192,2,8]{2,1,0:T(2,128)(2,1)} %bitcast.166) | data formatting | bytes 524288
  172.0 3.9 %all_to_all.63 = bf16[2,2,32768]{2,1,0:T(2,128)(2,1)S(1)} all-to-all(bf16[2,2,32768]{2,1,0:T(2,128)(2,1)S(1)} %reshape.244), channel_id=1, replica_groups=mesh['grp'=2,'path'=8,'amp'=2] {'amp'}, dimensions={0} | all-to-all | bytes 524288 | tf_op jit(solution)/shard_map/all_to_all | solution.py:136
  175.9 6.2 %reshape.245 = bf16[8192,2,8]{2,1,0:T(2,128)(2,1)} reshape(bf16[2,2,32768]{2,1,0:T(2,128)(2,1)S(1)} %all_to_all.63) | data formatting | bytes 524288
  182.1 9.3 %copy.82 = bf16[2,8,2,4096]{3,1,0,2:T(8,128)(2,1)} copy(bf16[2,8,2,4096]{1,2,3,0:T(2,128)(2,1)} %bitcast.167) | data formatting | bytes 524288 | tf_op jit(solution)/shard_map/all_to_all | solution.py:136
  191.4 1.8 copy.68
  193.4 46.4 %all-gather.5.cloned.1.call-done = bf16[128,2,4096]{2,0,1:T(8,128)(2,1)} async-done(((bf16[16,2,4096]{2,0,1:T(8,128)(2,1)}), bf16[128,2,4096]{2,0,1:T(8,128)(2,1)}) %all-gather.5.cloned.1.call-update) | async-done | bytes 2097168 | tf_op jit(solution)/shard_map/all_gather | solution.py:137
  239.8 1.7 slice_bitcast_fusion
  241.5 8.1 %convert_bitcast_fusion = bf16[1,2048,4096]{2,1,0:T(8,128)(2,1)} fusion(bf16[128,4096]{1,0:T(8,128)(2,1)S(1)} %get-tuple-element.14, bf16[128,4096]{1,0:T(8,128)(2,1)S(1)} %get-tuple-element.13, bf16[128,2048]{1,0:T(8,128)(2,1)S(1)} %get-tuple-element.16, bf16[128,2048]{1,0:T(8,128)(2,1)S(1)} %get-tuple-element.15), kind=kOutput, calls=%fused_computation.1 | convolution fusion | flops 4309647360 | bytes 19922944 | tf_op jit(solution)/shard_map/dot_general | solution.py:99
  249.6 1.3 fusion.82
  250.9 8.1 %convert_bitcast_fusion.1 = bf16[1,2048,4096]{2,1,0:T(8,128)(2,1)} fusion(bf16[128,4096]{1,0:T(8,128)(2,1)S(1)} %fusion.82, bf16[128,4096]{1,0:T(8,128)(2,1)S(1)} %get-tuple-element.14, bf16[128,2048]{1,0:T(8,128)(2,1)S(1)} %get-tuple-element.16, bf16[128,2048]{1,0:T(8,128)(2,1)S(1)} %get-tuple-element.15), kind=kOutput, calls=%fused_computation.2 | convolution fusion | flops 4309647360 | bytes 19922944 | tf_op jit(solution)/shard_map/dot_general | solution.py:96
  259.0 23.0 %pad_maximum_fusion = bf16[2,2048,4096]{2,1,0:T(8,128)(2,1)} fusion(bf16[1,2048,4096]{2,1,0:T(8,128)(2,1)} %convert_bitcast_fusion, bf16[1,2048,4096]{2,1,0:T(8,128)(2,1)} %convert_bitcast_fusion.1), kind=kLoop, calls=%fused_computation | loop fusion | flops 16777216 | bytes 67108864 | tf_op jit(solution)/shard_map/stack | solution.py:139
  (72 shorter events, 13.5 us)
Async XLA Ops:
  6.5 1.6 copy-start
  40.6 9.7 %copy-start.2 = (bf16[2,2,128,128]{3,2,1,0:T(8,128)(2,1)S(1)}, bf16[2,2,128,128]{3,2,1,0:T(8,128)(2,1)}, u32[]{:S(2)}) copy-start(bf16[2,2,128,128]{3,2,1,0:T(8,128)(2,1)} %param.13) | copy-start | bytes 393220
  40.6 9.7 %copy-start.3 = (bf16[16,2,4096]{2,1,0:T(2,128)(2,1)S(1)}, bf16[16,2,4096]{2,1,0:T(2,128)(2,1)}, u32[]{:S(2)}) copy-start(bf16[16,2,4096]{2,1,0:T(2,128)(2,1)} %param.8) | copy-start | bytes 786436
  40.6 9.9 %slice-start = ((bf16[2,2,128,128]{3,2,1,0:T(8,128)(2,1)}), bf16[1,2,128,128]{3,2,1,0:T(8,128)(2,1)S(1)}, s32[]{:S(2)}) async-start(bf16[2,2,128,128]{3,2,1,0:T(8,128)(2,1)} %param.13), calls=%async_computation.6 | async-start | bytes 131072 | tf_op jit(solution)/shard_map/slice | solution.py:135
  45.8 37.4 %all-to-all-start = ((bf16[16,2,8192]{2,1,0:T(2,128)(2,1)}), bf16[16,2,8192]{2,1,0:T(2,128)(2,1)S(1)}, u32[]{:S(2)}, u32[]{:S(2)}) async-start(bf16[16,2,8192]{2,1,0:T(2,128)(2,1)} %pad_maximum_fusion.4), calls=%async_computation | async-start | bytes 1048576 | tf_op jit(solution)/shard_map/all_to_all | solution.py:118
  83.2 28.9 %all-to-all-start.2 = ((bf16[16,2,4096]{2,1,0:T(2,128)(2,1)}), bf16[16,2,4096]{2,1,0:T(2,128)(2,1)S(1)}, u32[]{:S(2)}, u32[]{:S(2)}) async-start(bf16[16,2,4096]{2,1,0:T(2,128)(2,1)} %pad_maximum_fusion.5), calls=%async_computation.2 | async-start | bytes 524288 | tf_op jit(solution)/shard_map/all_to_all | solution.py:134
  112.1 22.5 %all-to-all-start.1 = ((bf16[8,2,16384]{2,1,0:T(2,128)(2,1)}), bf16[8,2,16384]{2,1,0:T(2,128)(2,1)S(1)}, u32[]{:S(2)}, u32[]{:S(2)}) async-start(bf16[8,2,16384]{2,1,0:T(2,128)(2,1)} %reshape.246), calls=%async_computation.1 | async-start | bytes 1048576 | tf_op jit(solution)/shard_map/all_to_all | solution.py:126
  119.4 72.0 %all-gather.3.cloned.1.call-start = ((), (), s32[]{:S(2)}) async-start(), calls=%async_computation.4 | async-start | bytes 1572864 | tf_op jit(solution)/shard_map/all_gather | solution.py:129
  158.0 81.8 %all-gather.5.cloned.1.call-start = ((), (), s32[]{:S(2)}) async-start(), calls=%async_computation.5 | async-start | bytes 2359296 | tf_op jit(solution)/shard_map/all_gather | solution.py:137
  259.0 23.0 %copy-start.1 = (f32[4,2,2,2]{0,3,2,1:T(2,128)S(1)}, f32[4,2,2,2]{0,3,2,1:T(2,128)}, u32[]{:S(2)}) copy-start(f32[4,2,2,2]{0,3,2,1:T(2,128)} %param.10) | copy-start | bytes 388
Sparse Core Ops, SparseCore 0:
  158.1 8.0 all-gather.2
  191.5 48.2 all-gather.4
where the time goes:
time: 290 us; the launch traced here: 289 us
  local copies, waits for them, and re-layouts  123 us (42%)
  waiting for transfers between devices  59.4 us (20%)
  other arithmetic  48.2 us (17%)
  matrix products  25.9 us (9%)
  starting transfers between devices  14.7 us (5%)
  between operations  13.9 us (5%)
  blocking collectives  3.94 us (1%)
    all_gather x1, waiting for transfers between devices, shards(): everything = lax.all_gather(right, 'path', axis=0, tiled=True)  46.4 us
    unnamed x12, local copies, waits for them, and re-layouts  34.3 us
    another operation x1, other arithmetic, shards(): return jnp.stack([real_part, imag_part], 0).astype(jnp.bfloat16)  23 us
    reshape x4, local copies, waits for them, and re-layouts, expand(): jnp.einsum('ab,nmj->najbm', identity, part)  20.9 us
    dot_general x1, other arithmetic, expand(): jnp.einsum('ab,nmj->najbm', identity, part)  18.8 us
    reshape x2, local copies, waits for them, and re-layouts, shards(): turned = turned.astype(jnp.bfloat16).reshape(half_paths, 2, full_left)  12.9 us
    all_to_all x1, waiting for transfers between devices, shards(): lax.all_to_all(turned, 'path', split_axis=2, concat_axis=0, tiled=True)  12.9 us
    all_to_all x1, local copies, waits for them, and re-layouts, shards(): lax.all_to_all(turned, 'path', split_axis=2, concat_axis=0, tiled=True)  12.5 us
  transfers between devices with their start and end apart: 5, of which 2 were waited for; matrix products, arithmetic and copies ran while one was open for 32% of the time, Pallas kernels for 0%

commit v1 on v0

--- a/solution.py
+++ b/solution.py
@@ -123,7 +123,10 @@
         moved.reshape(half_paths, 2 * gate_width, full_left // gate_width),
     )
     turned = turned.astype(jnp.bfloat16).reshape(half_paths, 2, full_left)
-    portion = lax.all_to_all(turned, "path", split_axis=2, concat_axis=0, tiled=True)
+    portion = jnp.concatenate(
+        lax.all_to_all(jnp.stack(jnp.split(turned, lax.axis_size("path"), axis=2)), "path", 0, 0),
+        axis=0,
+    )
     rows_here = portion.shape[2]
     portion = portion.reshape(path_count, half_paths, 2, rows_here)
     row_block = lax.all_gather(portion, "amp", axis=1, tiled=True).reshape(

time: 290 us -> 249 us (0.86)
  local copies, waits for them, and re-layouts: 123 us -> 81.4 us
    unnamed x12 -> x19, local copies, waits for them, and re-layouts: 34.3 us -> 17.8 us
    reshape x2 -> x1, local copies, waits for them, and re-layouts: 12.9 us -> 0.12 us  [shards(): turned = turned.astype(jnp.bfloat16).reshape(half_paths, 2, full_left)]
    all_to_all x1 -> x0, local copies, waits for them, and re-layouts: 12.5 us -> none  [shards(): lax.all_to_all(turned, 'path', split_axis=2, concat_axis=0, tiled=True)]
  transfers between devices with their start and end apart: 5 -> 5, of which waited for: 2 -> 2; matrix products, arithmetic and copies ran while one was open for 32% -> 30% of each run, Pallas kernels for 0% -> 0%
where the time goes in v1:
time: 249 us; the launch traced here: 248 us
  local copies, waits for them, and re-layouts  81.4 us (33%)
  waiting for transfers between devices  59.6 us (24%)
  other arithmetic  48.2 us (19%)
  matrix products  26.1 us (10%)
  starting transfers between devices  14.7 us (6%)
  between operations  13.9 us (6%)
  blocking collectives  3.94 us (2%)
    all_gather x1, waiting for transfers between devices, shards(): everything = lax.all_gather(right, 'path', axis=0, tiled=True)  46.6 us
    another operation x1, other arithmetic, shards(): return jnp.stack([real_part, imag_part], 0).astype(jnp.bfloat16)  23 us
    reshape x4, local copies, waits for them, and re-layouts, expand(): jnp.einsum('ab,nmj->najbm', identity, part)  20.9 us
    dot_general x1, other arithmetic, expand(): jnp.einsum('ab,nmj->najbm', identity, part)  18.8 us
    unnamed x19, local copies, waits for them, and re-layouts  17.8 us
    all_to_all x1, waiting for transfers between devices, shards(): lax.all_to_all(jnp.stack(jnp.split(turned, lax.axis_size('path'), axis=2)...  12.9 us
    another operation x1, local copies, waits for them, and re-layouts, right_high(): blocks = gate_mat.reshape(2, low_width, 2, low_width, 2)  10 us
    all_to_all x1, local copies, waits for them, and re-layouts, shards(): lax.all_to_all(right_turned, 'amp', split_axis=2, concat_axis=0, tiled=True)  9.3 us
  transfers between devices with their start and end apart: 5, of which 2 were waited for; matrix products, arithmetic and copies ran while one was open for 30% of the time, Pallas kernels for 0%

profile of v1, /device:TPU:0, one launch (start us, length us, event | category | flops | bytes accessed | tf_op | source)
XLA Modules:
  0.0 247.9 jit_solution(8860731851766736026)
XLA Ops:
  6.5 0.8 fusion.88
  7.3 0.8 slice_bitcast_fusion.28
  8.1 0.8 fusion.76
  9.0 0.8 fusion.74
  9.8 1.4 reshape.232
  11.3 18.8 %broadcast_multiply_fusion.3 = (f32[16,2,2,64,64]{0,1,4,2,3:T(2,128)}, f32[16,2,2,64,64]{0,1,4,2,3:T(2,128)}, f32[16,2,2,64,64]{0,1,4,2,3:T(2,128)}, f32[16,2,2,64,64]{0,1,4,2,3:T(2,128)}) fusion(f32[64,64]{1,0:T(8,128)S(1)} %fusion.69, f32[16,2,2]{0,1,2:T(2,128)S(1)} %copy.56, f32[16,2,2]{0,1,2:T(2,128)S(1)} %copy.59, f32[16,2,2]{0,1,2:T(2,128)S(1)} %copy.67, ...), kind=kLoop, calls=%fused_computation.6 | loop fusion | flops 1048576 | bytes 4211712 | tf_op jit(solution)/shard_map/ab,nmj->najbm/dot_general | solution.py:14
  30.1 5.2 %copy.58 = f32[16,128,128]{2,1,0:T(8,128)S(1)} copy(f32[16,128,128]{0,2,1:T(8,128)} %bitcast.191) | data formatting | bytes 2097152 | tf_op jit(solution)/shard_map/reshape | solution.py:14
  35.3 5.2 %copy.60 = f32[16,128,128]{2,1,0:T(8,128)S(1)} copy(f32[16,128,128]{0,2,1:T(8,128)} %bitcast.190) | data formatting | bytes 2097152 | tf_op jit(solution)/shard_map/reshape | solution.py:14
  43.8 2.0 pad_maximum_fusion.4
  45.8 3.7 %all-to-all-start = ((bf16[16,2,8192]{2,1,0:T(2,128)(2,1)}), bf16[16,2,8192]{2,1,0:T(2,128)(2,1)S(1)}, u32[]{:S(2)}, u32[]{:S(2)}) async-start(bf16[16,2,8192]{2,1,0:T(2,128)(2,1)} %pad_maximum_fusion.4), calls=%async_computation | async-start | bytes 1048576 | tf_op jit(solution)/shard_map/all_to_all | solution.py:118
  49.5 0.8 fusion.87
  50.5 10.0 %reshape_squeeze.17 = bf16[2,64,2,64,2]{4,3,2,1,0:T(8,128)(2,1)} reshape(bf16[1,2,128,128]{3,2,1,0:T(8,128)(2,1)S(1)} %slice-done) | data formatting | bytes 131072 | tf_op jit(solution)/shard_map/reshape;squeeze | solution.py:70
  60.6 7.9 %slice_reduce_fusion = (bf16[64,64]{1,0:T(8,128)(2,1)S(1)}, bf16[64,64]{1,0:T(8,128)(2,1)S(1)}, bf16[64,64]{1,0:T(8,128)(2,1)S(1)}, bf16[64,64]{1,0:T(8,128)(2,1...) fusion(bf16[2,64,2,64,2]{4,3,2,1,0:T(8,128)(2,1)} %reshape_sque, ...), kind=kLoop, calls=%fused_computation.34 | loop fusion | bytes 131072 | tf_op jit(solution)/shard_map/slice | solution.py:53
  68.6 5.2 %copy.69 = f32[16,128,128]{2,1,0:T(8,128)S(1)} copy(f32[16,128,128]{0,2,1:T(8,128)} %bitcast.189) | data formatting | bytes 2097152 | tf_op jit(solution)/shard_map/reshape | solution.py:14
  73.8 5.2 %copy.71 = f32[16,128,128]{2,1,0:T(8,128)S(1)} copy(f32[16,128,128]{0,2,1:T(8,128)} %bitcast.188) | data formatting | bytes 2097152 | tf_op jit(solution)/shard_map/reshape | solution.py:14
  81.9 1.3 pad_maximum_fusion.5
  83.2 3.4 %all-to-all-start.2 = ((bf16[16,2,4096]{2,1,0:T(2,128)(2,1)}), bf16[16,2,4096]{2,1,0:T(2,128)(2,1)S(1)}, u32[]{:S(2)}, u32[]{:S(2)}) async-start(bf16[16,2,4096]{2,1,0:T(2,128)(2,1)} %pad_maximum_fusion.5), calls=%async_computation.2 | async-start | bytes 524288 | tf_op jit(solution)/shard_map/all_to_all | solution.py:137
  93.6 7.3 %all-to-all-start.1 = ((bf16[8,8,2,2048]{3,2,1,0:T(2,128)(2,1)}), bf16[8,8,2,2048]{3,2,1,0:T(2,128)(2,1)S(1)}, u32[]{:S(2)}, u32[]{:S(2)}) async-start(bf16[8,8,2,2048]{3,2,1,0:T(2,128)(2,1)} %fusion.45), calls=%async_computation.1 | async-start | bytes 1048576 | tf_op jit(solution)/shard_map/all_to_all | solution.py:127
  103.1 12.9 %all-to-all-done.1 = bf16[8,8,2,2048]{3,2,1,0:T(2,128)(2,1)S(1)} async-done(((bf16[8,8,2,2048]{3,2,1,0:T(2,128)(2,1)}), bf16[8,8,2,2048]{3,2,1,0:T(2,128)(2,1)S(1)}, u32[]{:S(2)}, u32[]{:S(2)}) %all-to-all-start.1) | async-done | bytes 524320 | tf_op jit(solution)/shard_map/all_to_all | solution.py:127
  116.0 0.8 copy-done.2
  118.0 6.8 %copy.78 = bf16[8,2,8192]{0,1,2:T(2,128)(2,1)} copy(bf16[8,2,8192]{2,1,0:T(2,128)(2,1)S(1)} %reshape.230) | data formatting | bytes 524288 | tf_op jit(solution)/shard_map/reshape | solution.py:88
  124.7 6.1 %reshape.242 = bf16[2,2,32768]{2,1,0:T(2,128)(2,1)S(1)} reshape(bf16[8192,2,8]{2,1,0:T(2,128)(2,1)} %bitcast.192) | data formatting | bytes 524288
  130.9 3.9 %all_to_all.53 = bf16[2,2,32768]{2,1,0:T(2,128)(2,1)S(1)} all-to-all(bf16[2,2,32768]{2,1,0:T(2,128)(2,1)S(1)} %reshape.242), channel_id=1, replica_groups=mesh['grp'=2,'path'=8,'amp'=2] {'amp'}, dimensions={0} | all-to-all | bytes 524288 | tf_op jit(solution)/shard_map/all_to_all | solution.py:139
  134.8 6.2 %reshape.243 = bf16[8192,2,8]{2,1,0:T(2,128)(2,1)} reshape(bf16[2,2,32768]{2,1,0:T(2,128)(2,1)S(1)} %all_to_all.53) | data formatting | bytes 524288
  141.0 9.3 %copy.80 = bf16[2,8,2,4096]{3,1,0,2:T(8,128)(2,1)} copy(bf16[2,8,2,4096]{1,2,3,0:T(2,128)(2,1)} %bitcast.193) | data formatting | bytes 524288 | tf_op jit(solution)/shard_map/all_to_all | solution.py:139
  150.3 1.6 copy.66
  152.0 46.6 %all-gather.5.cloned.1.call-done = bf16[128,2,4096]{2,0,1:T(8,128)(2,1)} async-done(((bf16[16,2,4096]{2,0,1:T(8,128)(2,1)}), bf16[128,2,4096]{2,0,1:T(8,128)(2,1)}) %all-gather.5.cloned.1.call-update) | async-done | bytes 2097168 | tf_op jit(solution)/shard_map/all_gather | solution.py:140
  198.7 1.7 slice_bitcast_fusion
  200.3 8.2 %convert_bitcast_fusion = bf16[1,2048,4096]{2,1,0:T(8,128)(2,1)} fusion(bf16[128,4096]{1,0:T(8,128)(2,1)S(1)} %get-tuple-element.14, bf16[128,4096]{1,0:T(8,128)(2,1)S(1)} %get-tuple-element.13, bf16[128,2048]{1,0:T(8,128)(2,1)S(1)} %get-tuple-element.16, bf16[128,2048]{1,0:T(8,128)(2,1)S(1)} %get-tuple-element.15), kind=kOutput, calls=%fused_computation.1 | convolution fusion | flops 4309647360 | bytes 19922944 | tf_op jit(solution)/shard_map/dot_general | solution.py:99
  208.5 1.3 fusion.90
  209.8 8.2 %convert_bitcast_fusion.1 = bf16[1,2048,4096]{2,1,0:T(8,128)(2,1)} fusion(bf16[128,4096]{1,0:T(8,128)(2,1)S(1)} %fusion.90, bf16[128,4096]{1,0:T(8,128)(2,1)S(1)} %get-tuple-element.14, bf16[128,2048]{1,0:T(8,128)(2,1)S(1)} %get-tuple-element.16, bf16[128,2048]{1,0:T(8,128)(2,1)S(1)} %get-tuple-element.15), kind=kOutput, calls=%fused_computation.2 | convolution fusion | flops 4309647360 | bytes 19922944 | tf_op jit(solution)/shard_map/dot_general | solution.py:96
  218.1 23.0 %pad_maximum_fusion = bf16[2,2048,4096]{2,1,0:T(8,128)(2,1)} fusion(bf16[1,2048,4096]{2,1,0:T(8,128)(2,1)} %convert_bitcast_fusion, bf16[1,2048,4096]{2,1,0:T(8,128)(2,1)} %convert_bitcast_fusion.1), kind=kLoop, calls=%fused_computation | loop fusion | flops 16777216 | bytes 67108864 | tf_op jit(solution)/shard_map/stack | solution.py:142
  (78 shorter events, 16.6 us)
Async XLA Ops:
  6.5 1.6 copy-start
  42.5 7.8 %copy-start.3 = (bf16[2,2,128,128]{3,2,1,0:T(8,128)(2,1)S(1)}, bf16[2,2,128,128]{3,2,1,0:T(8,128)(2,1)}, u32[]{:S(2)}) copy-start(bf16[2,2,128,128]{3,2,1,0:T(8,128)(2,1)} %param.13) | copy-start | bytes 393220
  42.5 7.8 %copy-start.4 = (bf16[16,2,4096]{2,1,0:T(2,128)(2,1)S(1)}, bf16[16,2,4096]{2,1,0:T(2,128)(2,1)}, u32[]{:S(2)}) copy-start(bf16[16,2,4096]{2,1,0:T(2,128)(2,1)} %param.8) | copy-start | bytes 786436
  43.1 7.4 %slice-start = ((bf16[2,2,128,128]{3,2,1,0:T(8,128)(2,1)}), bf16[1,2,128,128]{3,2,1,0:T(8,128)(2,1)S(1)}, s32[]{:S(2)}) async-start(bf16[2,2,128,128]{3,2,1,0:T(8,128)(2,1)} %param.13), calls=%async_computation.6 | async-start | bytes 131072 | tf_op jit(solution)/shard_map/slice | solution.py:138
  45.8 37.4 %all-to-all-start = ((bf16[16,2,8192]{2,1,0:T(2,128)(2,1)}), bf16[16,2,8192]{2,1,0:T(2,128)(2,1)S(1)}, u32[]{:S(2)}, u32[]{:S(2)}) async-start(bf16[16,2,8192]{2,1,0:T(2,128)(2,1)} %pad_maximum_fusion.4), calls=%async_computation | async-start | bytes 1048576 | tf_op jit(solution)/shard_map/all_to_all | solution.py:118
  83.2 10.4 %all-to-all-start.2 = ((bf16[16,2,4096]{2,1,0:T(2,128)(2,1)}), bf16[16,2,4096]{2,1,0:T(2,128)(2,1)S(1)}, u32[]{:S(2)}, u32[]{:S(2)}) async-start(bf16[16,2,4096]{2,1,0:T(2,128)(2,1)} %pad_maximum_fusion.5), calls=%async_computation.2 | async-start | bytes 524288 | tf_op jit(solution)/shard_map/all_to_all | solution.py:137
  93.6 22.5 %all-to-all-start.1 = ((bf16[8,8,2,2048]{3,2,1,0:T(2,128)(2,1)}), bf16[8,8,2,2048]{3,2,1,0:T(2,128)(2,1)S(1)}, u32[]{:S(2)}, u32[]{:S(2)}) async-start(bf16[8,8,2,2048]{3,2,1,0:T(2,128)(2,1)} %fusion.45), calls=%async_computation.1 | async-start | bytes 1048576 | tf_op jit(solution)/shard_map/all_to_all | solution.py:127
  100.9 49.4 %all-gather.3.cloned.1.call-start = ((), (), s32[]{:S(2)}) async-start(), calls=%async_computation.4 | async-start | bytes 1572864 | tf_op jit(solution)/shard_map/all_gather | solution.py:132
  116.0 0.8 copy-start.2
  116.9 81.8 %all-gather.5.cloned.1.call-start = ((), (), s32[]{:S(2)}) async-start(), calls=%async_computation.5 | async-start | bytes 2359296 | tf_op jit(solution)/shard_map/all_gather | solution.py:140
  218.1 23.0 %copy-start.1 = (f32[4,2,2,2]{0,3,2,1:T(2,128)S(1)}, f32[4,2,2,2]{0,3,2,1:T(2,128)}, u32[]{:S(2)}) copy-start(f32[4,2,2,2]{0,3,2,1:T(2,128)} %param.10) | copy-start | bytes 388
Sparse Core Ops, SparseCore 0:
  117.0 8.0 all-gather.2
  150.4 48.2 all-gather.4
